TPU v7x, 256 devices: a whole 4x4x8 slice. The times are simulated.
256 devices in a mesh: row: 8 (over y, z_lo), col: 8 (over z_hi, core), layer: 4 (over x).
Axes of the slice: x: 4, y: 4, z: 8 (z_hi: 4, z_lo: 2; z = z_hi * 2 + z_lo), core: 2. Of those that a mesh axis runs over, the one named last changes fastest.
Arguments:
- density_tiles: bfloat16 [192, 8, 2, 128, 128], P(('row', 'col')), may hold values from -1.5 to 1.5
- tile_columns: int32 [192, 8, 2], P(('row', 'col')), may hold values from -1 to 191, as said below
Outputs:
- square_tiles: bfloat16 [192, 8, 2, 128, 128], P(('row', 'col'), None, None, 'layer')
Inputs may be any that keep to these rules, and one draw needn't show every extreme that they name: `tile_columns`: entry [i, g, s] is a tile column in group g (columns g * 24 to (g + 1) * 24 - 1) or -1; within one block row and group the listed columns are distinct and empty slots come after the listed ones; block row i lists its own column i in the first slot of its group, whose 2 slots are all listed; other groups hold 0 to 2 listed tiles.
All inputs are finite; a program needn't handle non-finite values.
Results may differ from a plain program's by a relative error of at most 0.0048.
Values may be sent and summed in bfloat16 or wider, within the bound.
No kernel may reach another device: no remote copies, remote signals or barrier semaphores. Data moves between devices by JAX's collectives and lax.ppermute only.
A program may use at most 64 MiB of HBM per device.

v0:
```python
import jax
import jax.numpy as jnp
from jax import lax
from jax.sharding import Mesh
from jax.sharding import PartitionSpec as P

ROW = ("row_0", "row_1")
ROW_COL = ("row_0", "row_1", "col")


def filled_up(lines, devices):
    spare = -len(lines) % devices
    return jnp.pad(lines, [(0, spare)] + [(0, 0)] * (lines.ndim - 1))


def spread(array, axis, root):
    lines = jnp.where(lax.axis_index(axis) == root, array, jnp.zeros_like(array)).reshape(
        -1, *array.shape[1:][-1:]
    )
    padded = filled_up(lines, lax.axis_size(axis))
    own = lax.psum_scatter(padded, axis, scatter_dimension=0, tiled=True)
    return lax.all_gather(own, axis, axis=0, tiled=True)[: len(lines)].reshape(array.shape)


def broadcast_by_axis(array, axes, root):
    array = jnp.where(lax.axis_index(axes) == root, array, jnp.zeros_like(array))
    for axis in axes:
        array = lax.psum(array, axis)
    return array


def in_blocks(array, dim, devices):
    before, after = (array.shape[:dim], array.shape[dim + 1 :])
    return jnp.moveaxis(array.reshape(*before, devices, -1, *after), dim, 0)


def sent_and_summed(array, axis, dim):
    pieces = in_blocks(array, dim, lax.axis_size(axis))
    arrived = lax.all_to_all(pieces, axis, split_axis=0, concat_axis=0, tiled=True)
    return arrived.astype(jnp.float32).sum(axis=0)


def multiply(left_tiles, left_columns, right_tiles, right_columns, target_columns, start_row):
    is_live = left_columns >= 0
    inner_rows = jnp.where(is_live, left_columns - start_row, 0).astype(jnp.int32)
    inner_columns = right_columns[inner_rows]
    matches = (
        (inner_columns[:, :, None, :] == target_columns[:, None, :, None])
        & is_live[:, :, None, None]
        & (target_columns >= 0)[:, None, :, None]
    )
    slot_index = jnp.argmax(matches.astype(jnp.int32), axis=-1)
    located = jnp.any(matches, axis=-1)
    selected = right_tiles[inner_rows[:, :, None], slot_index]
    selected = jnp.where(located[:, :, :, None, None], selected, jnp.zeros((), jnp.bfloat16))
    return jnp.einsum("iarc,iascd->isrd", left_tiles, selected, preferred_element_type=jnp.float32)


def on_device(density_tiles, tile_columns):
    row_count = lax.axis_size(ROW)
    column_count = lax.axis_size("col")
    layer_count = lax.axis_size("layer")
    grid_tiles, grid_columns = (
        lax.all_to_all(density_tiles, "col", split_axis=1, concat_axis=0, tiled=True),
        lax.all_to_all(tile_columns, "col", split_axis=1, concat_axis=0, tiled=True),
    )
    block_tiles = grid_tiles[:, 0]
    block_columns = grid_columns[:, 0]
    group_rows = block_tiles.shape[0]
    row_ratio = column_count // row_count
    panel_rows = group_rows // row_ratio
    per_layer = column_count // layer_count
    layer_index = lax.axis_index("layer")
    partial_value = jnp.zeros(block_tiles.shape, jnp.float32)
    for panel_step in range(per_layer):
        panel_index = layer_index * per_layer + panel_step
        left_tiles, left_columns = (
            spread(block_tiles, "col", panel_index),
            spread(block_columns, "col", panel_index),
        )
        right_tiles, right_columns = (
            broadcast_by_axis(block_tiles, ROW, panel_index // row_ratio),
            broadcast_by_axis(block_columns, ROW, panel_index // row_ratio),
        )
        partial_value = partial_value + multiply(
            left_tiles,
            left_columns,
            right_tiles,
            right_columns,
            block_columns,
            panel_index * panel_rows,
        )
    rounded = partial_value.astype(jnp.bfloat16)
    summed = sent_and_summed(rounded.astype(jnp.float32).astype(jnp.bfloat16), "layer", 2)
    returned = lax.all_to_all(
        summed.astype(jnp.bfloat16)[:, None], "col", split_axis=0, concat_axis=1, tiled=True
    )
    return returned


def solution(mesh):
    split = Mesh(
        mesh.devices.reshape(4, 2, mesh.shape["col"], mesh.shape["layer"]),
        ("row_0", "row_1", "col", "layer"),
    )
    return jax.shard_map(
        on_device,
        mesh=split,
        in_specs=(P(ROW_COL, None, None, None, None), P(ROW_COL, None, None)),
        out_specs=P(ROW_COL, None, None, "layer", None),
        check_vma=False,
    )
```

profile of v0, /device:TPU:1, one launch (start us, length us, event | category | flops | bytes accessed | tf_op | source)
XLA Modules:
  0.0 319.0 jit_solution(11141987187466286460)
XLA Ops:
  7.4 2.7 copy.204
  10.1 10.0 %all-to-all-start.1 = ((bf16[3,8,2,128,128]{4,3,2,0,1:T(8,128)(2,1)}), bf16[3,8,2,128,128]{4,3,2,0,1:T(8,128)(2,1)S(1)}, u32[]{:S(2)}, u32[]{:S(2)}) async-start(bf16[3,8,2,128,128]{4,3,2,0,1:T(8,128)(2,1)} %copy.204), calls=%async_computation.1 | async-start | bytes 3145728 | tf_op jit(solution)/shard_map/all_to_all | solution.py:64
  20.1 33.3 %all-to-all-done.1 = bf16[3,8,2,128,128]{4,3,2,0,1:T(8,128)(2,1)S(1)} async-done(((bf16[3,8,2,128,128]{4,3,2,0,1:T(8,128)(2,1)}), bf16[3,8,2,128,128]{4,3,2,0,1:T(8,128)(2,1)S(1)}, u32[]{:S(2)}, u32[]{:S(2)}) %all-to-all-start.1) | async-done | bytes 1572896 | tf_op jit(solution)/shard_map/all_to_all | solution.py:64
  53.4 2.8 broadcast_select_fusion.2
  56.3 0.5 reduce-scatter.5.cloned.1.call-update
  56.8 0.5 reduce-scatter.3.cloned.1.call-update
  57.4 82.9 %all-reduce.10.cloned.1.call-done = (bf16[24,2,128,128]{3,2,1,0:T(8,128)(2,1)}, bf16[24,2,128,128]{3,2,1,0:T(8,128)(2,1)}) async-done(((bf16[24,2,128,128]{3,2,1,0:T(8,128)(2,1)}, bf16[24,2,128,128]{3,2,1,0:T(8,128)(2,1)}), (bf16[24,2,128,128]{3,2,1,0:T(8,128)(2,1)}, bf16[24,2,128,128]{3,2,1,0:T(8,128)(2,1)})) %all-reduce.10.cloned.1.call-update) | async-done | bytes 3145744 | tf_op jit(solution)/shard_map/psum | solution.py:28
  140.4 0.5 all-gather.7.cloned.1.call-update
  141.0 0.7 copy.187
  141.7 7.8 %all-to-all-start = ((s32[3,8,2]{0,2,1:T(2,128)}), s32[3,8,2]{0,2,1:T(2,128)S(1)}, u32[]{:S(2)}, u32[]{:S(2)}) async-start(s32[3,8,2]{0,2,1:T(2,128)} %copy.187), calls=%async_computation | async-start | bytes 16384 | tf_op jit(solution)/shard_map/all_to_all | solution.py:65
  149.5 0.6 dynamic-slice
  150.7 5.9 %all-to-all-done = s32[3,8,2]{0,2,1:T(2,128)S(1)} async-done(((s32[3,8,2]{0,2,1:T(2,128)}), s32[3,8,2]{0,2,1:T(2,128)S(1)}, u32[]{:S(2)}, u32[]{:S(2)}) %all-to-all-start) | async-done | bytes 224 | tf_op jit(solution)/shard_map/all_to_all | solution.py:65
  156.8 25.1 %all-reduce.2 = (s32[24,2]{1,0:T(8,128)S(1)}, s32[24,2]{1,0:T(8,128)S(1)}) all-reduce(s32[24,2]{1,0:T(8,128)S(1)} %get-tuple-element.32, s32[24,2]{1,0:T(8,128)S(1)} %get-tuple-element.34), channel_id=4, replica_groups=mesh['row_0'=4,'row_1'=2,'col'=8,'layer'=4] {'col'}, use_global_device_ids=true, to_apply=%region_10.11.clone | all-reduce | flops 96 | bytes 768
  181.9 0.1 copy.192
  182.0 12.9 %all-gather = s32[8,3,2]{1,2,0:T(2,128)S(1)} all-gather(s32[1,3,2]{1,2,0:T(2,128)S(1)} %bitcast.110), channel_id=1, replica_groups=mesh['row_0'=4,'row_1'=2,'col'=8,'layer'=4] {'col'}, dimensions={0}, use_global_device_ids=true | all-gather | bytes 216 | tf_op jit(solution)/shard_map/all_gather | solution.py:22
  195.1 0.1 copy.202
  195.2 0.1 copy.210
  195.3 0.1 copy.194
  195.5 0.1 copy.197
  195.7 13.0 %all-gather.1 = s32[8,3,2]{1,2,0:T(2,128)S(1)} all-gather(s32[1,3,2]{1,2,0:T(2,128)S(1)} %bitcast.109), channel_id=1, replica_groups=mesh['row_0'=4,'row_1'=2,'col'=8,'layer'=4] {'col'}, dimensions={0}, use_global_device_ids=true | all-gather | bytes 216 | tf_op jit(solution)/shard_map/all_gather | solution.py:22
  208.8 0.1 copy.212
  209.0 0.1 copy.215
  209.5 0.1 reshape.81
  209.6 13.5 %all-reduce.3 = (s32[24,2]{1,0:T(8,128)S(1)}, s32[24,2]{1,0:T(8,128)S(1)}) all-reduce(s32[24,2]{1,0:T(8,128)S(1)} %get-tuple-element.33, s32[24,2]{1,0:T(8,128)S(1)} %get-tuple-element.31), channel_id=1, replica_groups=mesh['row_0'=4,'row_1'=2,'col'=8,'layer'=4] {'row_0'}, use_global_device_ids=true, to_apply=%region_8.9 | all-reduce | flops 96 | bytes 768 | tf_op jit(solution)/shard_map/psum | solution.py:28
  223.0 7.7 %all-reduce.4 = (s32[24,2]{1,0:T(8,128)S(1)}, s32[24,2]{1,0:T(8,128)S(1)}) all-reduce(s32[24,2]{1,0:T(8,128)S(1)} %get-tuple-element.11, s32[24,2]{1,0:T(8,128)S(1)} %get-tuple-element.12), channel_id=1, replica_groups=mesh['row_0'=4,'row_1'=2,'col'=8,'layer'=4] {'row_1'}, use_global_device_ids=true, to_apply=%region_9.10 | all-reduce | flops 96 | bytes 768 | tf_op jit(solution)/shard_map/psum | solution.py:28
  230.7 0.6 gather_fusion.2
  231.3 0.1 copy.218
  231.6 0.1 reshape.67
  231.7 0.6 gather_fusion
  232.4 0.1 copy.203
  232.5 0.1 copy.219
  232.7 0.6 iota_reduce_fusion
  233.3 0.1 copy.221
  233.4 0.1 reshape.87
  233.5 0.6 iota_reduce_fusion.1
  234.2 0.1 copy.206
  234.3 0.1 reshape.73
  234.4 11.8 %all-reduce.12.cloned.1.call-done = (bf16[24,2,128,128]{3,2,1,0:T(8,128)(2,1)}, bf16[24,2,128,128]{3,2,1,0:T(8,128)(2,1)}) async-done(((bf16[24,2,128,128]{3,2,1,0:T(8,128)(2,1)}, bf16[24,2,128,128]{3,2,1,0:T(8,128)(2,1)}), (bf16[24,2,128,128]{3,2,1,0:T(8,128)(2,1)}, bf16[24,2,128,128]{3,2,1,0:T(8,128)(2,1)})) %all-reduce.12.cloned.1.call-update) | async-done | bytes 3145744 | tf_op jit(solution)/shard_map/psum | solution.py:28
  246.2 4.5 %gather_fusion.3 = bf16[96,128,128]{2,1,0:T(8,128)(2,1)} fusion(bf16[24,2,128,128]{3,2,1,0:T(8,128)(2,1)} %get-tuple-element.17, s32[96]{0:T(128)S(1)} %reshape.87), kind=kCustom, calls=%fused_computation.3 | custom fusion | bytes 6292224 | tf_op jit(solution)/shard_map/gather | solution.py:54
  250.6 3.0 gather_fusion.1
  253.7 4.8 %fusion.1 = f32[24,2,128,128,1]{2,3,1,4,0:T(8,128)} fusion(bf16[24,2,128,128,1]{3,2,4,1,0:T(8,128)(2,1)} %bitcast.105, bf16[24,2,2,128,128]{4,3,2,1,0:T(8,128)(2,1)} %bitcast.95, pred[24,2,2]{2,1,0:T(4,128)(4,1)S(1)} %copy.219), kind=kOutput, calls=%fused_computation.6 | convolution fusion | flops 404226048 | bytes 7864416 | tf_op jit(solution)/shard_map/iarc,iascd->isrd/dot_general | solution.py:56
  258.5 5.5 %all-gather.5.cloned.1.call-done = bf16[6144,128]{1,0:T(8,128)(2,1)} async-done(((bf16[768,128]{1,0:T(8,128)(2,1)}), bf16[6144,128]{1,0:T(8,128)(2,1)}) %all-gather.5.cloned.1.call-update) | async-done | bytes 1572880 | tf_op jit(solution)/shard_map/all_gather | solution.py:22
  263.9 3.0 fusion
  267.0 0.4 copy.235
  267.4 24.0 %all_to_all.47 = bf16[4,24,2,32,128]{4,3,2,1,0:T(8,128)(2,1)S(1)} all-to-all(bf16[4,24,2,32,128]{4,3,2,1,0:T(8,128)(2,1)S(1)} %bitcast.97), channel_id=1, replica_groups=mesh['row_0'=4,'row_1'=2,'col'=8,'layer'=4] {'layer'}, dimensions={0} | all-to-all | bytes 3145728 | tf_op jit(solution)/shard_map/all_to_all | solution.py:39
  291.4 0.3 reduce_sum.12
  291.8 18.9 %all_to_all.48 = bf16[24,1,2,32,128]{4,3,2,1,0:T(8,128)(2,1)S(1)} all-to-all(bf16[24,1,2,32,128]{4,3,2,1,0:T(8,128)(2,1)S(1)} %bitcast.104), channel_id=1, replica_groups=mesh['row_0'=4,'row_1'=2,'col'=8,'layer'=4] {'col'}, dimensions={0} | all-to-all | bytes 786432 | tf_op jit(solution)/shard_map/all_to_all | solution.py:95
  310.6 0.8 copy.224
  (46 shorter events, 1.8 us)
Async XLA Ops:
  10.1 43.3 %all-to-all-start.1 = ((bf16[3,8,2,128,128]{4,3,2,0,1:T(8,128)(2,1)}), bf16[3,8,2,128,128]{4,3,2,0,1:T(8,128)(2,1)S(1)}, u32[]{:S(2)}, u32[]{:S(2)}) async-start(bf16[3,8,2,128,128]{4,3,2,0,1:T(8,128)(2,1)} %copy.204), calls=%async_computation.1 | async-start | bytes 3145728 | tf_op jit(solution)/shard_map/all_to_all | solution.py:64
  20.1 120.3 %all-reduce.10.cloned.1.call-start = ((), (), s32[]{:S(2)}) async-start(), calls=%async_computation.10 | async-start | bytes 6291456 | tf_op jit(solution)/shard_map/psum | solution.py:28
  56.2 84.2 %reduce-scatter.5.cloned.1.call-start = ((), (), s32[]{:S(2)}) async-start(), calls=%async_computation.8 | async-start | bytes 1769472 | tf_op jit(solution)/shard_map/reduce_scatter | solution.py:21
  56.8 138.2 %reduce-scatter.3.cloned.1.call-start = ((), (), s32[]{:S(2)}) async-start(), calls=%async_computation.6 | async-start | bytes 1769472 | tf_op jit(solution)/shard_map/reduce_scatter | solution.py:21
  57.4 188.8 %all-reduce.12.cloned.1.call-start = ((), (), s32[]{:S(2)}) async-start(), calls=%async_computation.11 | async-start | bytes 6291456 | tf_op jit(solution)/shard_map/psum | solution.py:28
  140.3 0.7 copy-start
  140.3 9.2 %copy-start.1 = (u32[256]{0:T(256)S(1)}, u32[256]{0:T(256)}, u32[]{:S(2)}) copy-start(u32[256]{0:T(256)} %constant.100) | copy-start | bytes 3076
  140.3 113.3 %all-gather.7.cloned.1.call-start = ((), (), s32[]{:S(2)}) async-start(), calls=%async_computation.9 | async-start | bytes 1769472 | tf_op jit(solution)/shard_map/all_gather | solution.py:22
  141.7 14.9 %all-to-all-start = ((s32[3,8,2]{0,2,1:T(2,128)}), s32[3,8,2]{0,2,1:T(2,128)S(1)}, u32[]{:S(2)}, u32[]{:S(2)}) async-start(s32[3,8,2]{0,2,1:T(2,128)} %copy.187), calls=%async_computation | async-start | bytes 16384 | tf_op jit(solution)/shard_map/all_to_all | solution.py:65
  149.5 114.4 %all-gather.5.cloned.1.call-start = ((), (), s32[]{:S(2)}) async-start(), calls=%async_computation.7 | async-start | bytes 1769472 | tf_op jit(solution)/shard_map/all_gather | solution.py:22
Sparse Core Ops, SparseCore 0:
  56.3 83.9 all-reduce.9
  143.0 103.1 all-reduce.11
Sparse Core Ops, SparseCore 1:
  59.3 43.9 reduce-scatter.4
  105.7 40.1 reduce-scatter.2
  147.6 63.6 all-gather.6
  213.1 50.8 all-gather.4
where the time goes:
time: 319 us
  waiting for transfers between devices  141 us (44%)
  blocking collectives  115 us (36%)
  starting transfers between devices  18 us (6%)
  local copies, waits for them, and re-layouts  16.9 us (5%)
  between operations  15.8 us (5%)
  matrix products  7.82 us (2%)
  other arithmetic  4.51 us (1%)
    psum x2, waiting for transfers between devices, broadcast_by_axis(): array = lax.psum(array, axis)  94.7 us
    all_to_all x1, waiting for transfers between devices, on_device(): lax.all_to_all(density_tiles, 'col', split_axis=1, concat_axis=0, tiled=T...  33.3 us
    all_gather x2, blocking collectives, spread(): lax.all_gather(own, axis, axis=0, tiled=True)[:len(lines)]  25.9 us
    unnamed x1, blocking collectives  25.1 us
    all_to_all x1, blocking collectives, sent_and_summed(): lax.all_to_all(pieces, axis, split_axis=0, concat_axis=0, tiled=True)  24 us
    psum x2, blocking collectives, broadcast_by_axis(): array = lax.psum(array, axis)  21.2 us
    all_to_all x1, blocking collectives, on_device(): lax.all_to_all(summed.astype(jnp.bfloat16)[:, None], 'col', split_axis=0,...  18.9 us
    all_to_all x1, starting transfers between devices, on_device(): lax.all_to_all(density_tiles, 'col', split_axis=1, concat_axis=0, tiled=T...  9.95 us
  transfers between devices with their start and end apart: 8, of which 5 were waited for; matrix products, arithmetic and copies ran while one was open for 6% of the time, Pallas kernels for 0%

commit v1 on v0

--- a/solution.py
+++ b/solution.py
@@ -6,6 +6,12 @@
 
 ROW = ("row_0", "row_1")
 ROW_COL = ("row_0", "row_1", "col")
+
+
+def trade_parts(array, axis, split, join):
+    pieces = jnp.split(array, lax.axis_size(axis), axis=split)
+    received = lax.all_to_all(jnp.stack(pieces), axis, 0, 0)
+    return jnp.concatenate(received, axis=join)
 
 
 def filled_up(lines, devices):
@@ -61,7 +67,7 @@
     column_count = lax.axis_size("col")
     layer_count = lax.axis_size("layer")
     grid_tiles, grid_columns = (
-        lax.all_to_all(density_tiles, "col", split_axis=1, concat_axis=0, tiled=True),
+        trade_parts(density_tiles, "col", 1, 0),
         lax.all_to_all(tile_columns, "col", split_axis=1, concat_axis=0, tiled=True),
     )
     block_tiles = grid_tiles[:, 0]

time: 319 us -> 330 us (1.034)
  local copies, waits for them, and re-layouts: 16.9 us -> 27.1 us
    unnamed x8 -> x14, local copies, waits for them, and re-layouts: 4.1 us -> 12.6 us
where the time goes in v1:
time: 330 us; the launch traced here: 329 us
  waiting for transfers between devices  141 us (43%)
  blocking collectives  115 us (35%)
  local copies, waits for them, and re-layouts  27.1 us (8%)
  starting transfers between devices  18 us (5%)
  between operations  15.8 us (5%)
  matrix products  7.82 us (2%)
  other arithmetic  4.51 us (1%)
    psum x2, waiting for transfers between devices, broadcast_by_axis(): array = lax.psum(array, axis)  94.7 us
    all_to_all x1, waiting for transfers between devices, trade_parts(): received = lax.all_to_all(jnp.stack(pieces), axis, 0, 0)  33.3 us
    all_gather x2, blocking collectives, spread(): lax.all_gather(own, axis, axis=0, tiled=True)[:len(lines)]  25.9 us
    unnamed x1, blocking collectives  25.1 us
    all_to_all x1, blocking collectives, sent_and_summed(): lax.all_to_all(pieces, axis, split_axis=0, concat_axis=0, tiled=True)  24 us
    psum x2, blocking collectives, broadcast_by_axis(): array = lax.psum(array, axis)  21.2 us
    all_to_all x1, blocking collectives, on_device(): lax.all_to_all(summed.astype(jnp.bfloat16)[:, None], 'col', split_axis=0,...  18.9 us
    unnamed x14, local copies, waits for them, and re-layouts  12.6 us
  transfers between devices with their start and end apart: 8, of which 5 were waited for; matrix products, arithmetic and copies ran while one was open for 6% of the time, Pallas kernels for 0%

profile of v1, /device:TPU:1, one launch (start us, length us, event | category | flops | bytes accessed | tf_op | source)
XLA Modules:
  0.0 329.2 jit_solution(4951035234215629630)
XLA Ops:
  7.4 1.6 bitcast_dynamic-update-slice_fusion.6
  9.0 1.6 bitcast_dynamic-update-slice_fusion.5
  10.6 1.6 bitcast_dynamic-update-slice_fusion.4
  12.2 1.6 bitcast_dynamic-update-slice_fusion.3
  13.8 1.6 bitcast_dynamic-update-slice_fusion.2
  15.4 1.6 bitcast_dynamic-update-slice_fusion.7
  17.0 1.6 bitcast_dynamic-update-slice_fusion.1
  18.7 1.6 bitcast_dynamic-update-slice_fusion
  20.3 10.0 %all-to-all-start.1 = ((bf16[8,3,1,2,128,128]{5,4,3,1,2,0:T(8,128)(2,1)}), bf16[8,3,1,2,128,128]{5,4,3,1,2,0:T(8,128)(2,1)S(1)}, u32[]{:S(2)}, u32[]{:S(2)}) async-start(bf16[8,3,1,2,128,128]{5,4,3,1,2,0:T(8,128)(2,1)} %bitcast_dynamic-update-slice_fusion), calls=%async_computation.1 | async-start | bytes 3145728 | tf_op jit(solution)/shard_map/all_to_all | solution.py:13
  30.2 33.3 %all-to-all-done.1 = bf16[8,3,1,2,128,128]{5,4,3,1,2,0:T(8,128)(2,1)S(1)} async-done(((bf16[8,3,1,2,128,128]{5,4,3,1,2,0:T(8,128)(2,1)}), bf16[8,3,1,2,128,128]{5,4,3,1,2,0:T(8,128)(2,1)S(1)}, u32[]{:S(2)}, u32[]{:S(2)}) %all-to-all-start.1) | async-done | bytes 1572896 | tf_op jit(solution)/shard_map/all_to_all | solution.py:13
  63.6 2.8 broadcast_select_fusion.2
  66.5 0.5 reduce-scatter.5.cloned.1.call-update
  67.0 0.5 reduce-scatter.3.cloned.1.call-update
  67.6 82.9 %all-reduce.10.cloned.1.call-done = (bf16[24,2,128,128]{3,2,1,0:T(8,128)(2,1)}, bf16[24,2,128,128]{3,2,1,0:T(8,128)(2,1)}) async-done(((bf16[24,2,128,128]{3,2,1,0:T(8,128)(2,1)}, bf16[24,2,128,128]{3,2,1,0:T(8,128)(2,1)}), (bf16[24,2,128,128]{3,2,1,0:T(8,128)(2,1)}, bf16[24,2,128,128]{3,2,1,0:T(8,128)(2,1)})) %all-reduce.10.cloned.1.call-update) | async-done | bytes 3145744 | tf_op jit(solution)/shard_map/psum | solution.py:34
  150.6 0.5 all-gather.7.cloned.1.call-update
  151.2 0.7 copy.218
  151.9 7.8 %all-to-all-start = ((s32[3,8,2]{0,2,1:T(2,128)}), s32[3,8,2]{0,2,1:T(2,128)S(1)}, u32[]{:S(2)}, u32[]{:S(2)}) async-start(s32[3,8,2]{0,2,1:T(2,128)} %copy.218), calls=%async_computation | async-start | bytes 16384 | tf_op jit(solution)/shard_map/all_to_all | solution.py:71
  159.7 0.6 dynamic-slice
  160.9 5.9 %all-to-all-done = s32[3,8,2]{0,2,1:T(2,128)S(1)} async-done(((s32[3,8,2]{0,2,1:T(2,128)}), s32[3,8,2]{0,2,1:T(2,128)S(1)}, u32[]{:S(2)}, u32[]{:S(2)}) %all-to-all-start) | async-done | bytes 224 | tf_op jit(solution)/shard_map/all_to_all | solution.py:71
  166.9 25.1 %all-reduce.2 = (s32[24,2]{1,0:T(8,128)S(1)}, s32[24,2]{1,0:T(8,128)S(1)}) all-reduce(s32[24,2]{1,0:T(8,128)S(1)} %get-tuple-element.32, s32[24,2]{1,0:T(8,128)S(1)} %get-tuple-element.34), channel_id=4, replica_groups=mesh['row_0'=4,'row_1'=2,'col'=8,'layer'=4] {'col'}, use_global_device_ids=true, to_apply=%region_10.11.clone | all-reduce | flops 96 | bytes 768
  192.2 12.9 %all-gather = s32[8,3,2]{1,2,0:T(2,128)S(1)} all-gather(s32[1,3,2]{1,2,0:T(2,128)S(1)} %bitcast.124), channel_id=1, replica_groups=mesh['row_0'=4,'row_1'=2,'col'=8,'layer'=4] {'col'}, dimensions={0}, use_global_device_ids=true | all-gather | bytes 216 | tf_op jit(solution)/shard_map/all_gather | solution.py:28
  205.6 0.1 copy.228
  205.9 13.0 %all-gather.1 = s32[8,3,2]{1,2,0:T(2,128)S(1)} all-gather(s32[1,3,2]{1,2,0:T(2,128)S(1)} %bitcast.123), channel_id=1, replica_groups=mesh['row_0'=4,'row_1'=2,'col'=8,'layer'=4] {'col'}, dimensions={0}, use_global_device_ids=true | all-gather | bytes 216 | tf_op jit(solution)/shard_map/all_gather | solution.py:28
  219.0 0.1 copy.249
  219.2 0.1 copy.252
  219.7 13.5 %all-reduce.3 = (s32[24,2]{1,0:T(8,128)S(1)}, s32[24,2]{1,0:T(8,128)S(1)}) all-reduce(s32[24,2]{1,0:T(8,128)S(1)} %get-tuple-element.33, s32[24,2]{1,0:T(8,128)S(1)} %get-tuple-element.31), channel_id=1, replica_groups=mesh['row_0'=4,'row_1'=2,'col'=8,'layer'=4] {'row_0'}, use_global_device_ids=true, to_apply=%region_8.9 | all-reduce | flops 96 | bytes 768 | tf_op jit(solution)/shard_map/psum | solution.py:34
  233.2 7.7 %all-reduce.4 = (s32[24,2]{1,0:T(8,128)S(1)}, s32[24,2]{1,0:T(8,128)S(1)}) all-reduce(s32[24,2]{1,0:T(8,128)S(1)} %get-tuple-element.11, s32[24,2]{1,0:T(8,128)S(1)} %get-tuple-element.12), channel_id=1, replica_groups=mesh['row_0'=4,'row_1'=2,'col'=8,'layer'=4] {'row_1'}, use_global_device_ids=true, to_apply=%region_9.10 | all-reduce | flops 96 | bytes 768 | tf_op jit(solution)/shard_map/psum | solution.py:34
  240.9 0.6 gather_fusion.2
  241.9 0.6 gather_fusion
  242.6 0.1 copy.234
  242.7 0.1 copy.256
  242.8 0.6 iota_reduce_fusion
  243.5 0.1 copy.258
  243.6 0.1 reshape.74
  243.7 0.6 iota_reduce_fusion.1
  244.4 0.1 copy.243
  244.5 0.1 reshape.60
  244.6 11.8 %all-reduce.12.cloned.1.call-done = (bf16[24,2,128,128]{3,2,1,0:T(8,128)(2,1)}, bf16[24,2,128,128]{3,2,1,0:T(8,128)(2,1)}) async-done(((bf16[24,2,128,128]{3,2,1,0:T(8,128)(2,1)}, bf16[24,2,128,128]{3,2,1,0:T(8,128)(2,1)}), (bf16[24,2,128,128]{3,2,1,0:T(8,128)(2,1)}, bf16[24,2,128,128]{3,2,1,0:T(8,128)(2,1)})) %all-reduce.12.cloned.1.call-update) | async-done | bytes 3145744 | tf_op jit(solution)/shard_map/psum | solution.py:34
  256.4 4.5 %gather_fusion.3 = bf16[96,128,128]{2,1,0:T(8,128)(2,1)} fusion(bf16[24,2,128,128]{3,2,1,0:T(8,128)(2,1)} %get-tuple-element.17, s32[96]{0:T(128)S(1)} %reshape.74), kind=kCustom, calls=%fused_computation.3 | custom fusion | bytes 6292224 | tf_op jit(solution)/shard_map/gather | solution.py:60
  260.8 3.0 gather_fusion.1
  263.8 4.8 %fusion.1 = f32[24,2,128,128,1]{2,3,1,4,0:T(8,128)} fusion(bf16[24,2,128,128,1]{3,2,4,1,0:T(8,128)(2,1)} %bitcast.119, bf16[24,2,2,128,128]{4,3,2,1,0:T(8,128)(2,1)} %bitcast.109, pred[24,2,2]{2,1,0:T(4,128)(4,1)S(1)} %copy.256), kind=kOutput, calls=%fused_computation.6 | convolution fusion | flops 404226048 | bytes 7864416 | tf_op jit(solution)/shard_map/iarc,iascd->isrd/dot_general | solution.py:62
  268.6 5.5 %all-gather.5.cloned.1.call-done = bf16[6144,128]{1,0:T(8,128)(2,1)} async-done(((bf16[768,128]{1,0:T(8,128)(2,1)}), bf16[6144,128]{1,0:T(8,128)(2,1)}) %all-gather.5.cloned.1.call-update) | async-done | bytes 1572880 | tf_op jit(solution)/shard_map/all_gather | solution.py:28
  274.1 3.0 fusion
  277.2 0.4 copy.279
  277.6 24.0 %all_to_all.43 = bf16[4,24,2,32,128]{4,3,2,1,0:T(8,128)(2,1)S(1)} all-to-all(bf16[4,24,2,32,128]{4,3,2,1,0:T(8,128)(2,1)S(1)} %bitcast.111), channel_id=1, replica_groups=mesh['row_0'=4,'row_1'=2,'col'=8,'layer'=4] {'layer'}, dimensions={0} | all-to-all | bytes 3145728 | tf_op jit(solution)/shard_map/all_to_all | solution.py:45
  301.6 0.3 reduce_sum.12
  301.9 18.9 %all_to_all.44 = bf16[24,1,2,32,128]{4,3,2,1,0:T(8,128)(2,1)S(1)} all-to-all(bf16[24,1,2,32,128]{4,3,2,1,0:T(8,128)(2,1)S(1)} %bitcast.118), channel_id=1, replica_groups=mesh['row_0'=4,'row_1'=2,'col'=8,'layer'=4] {'col'}, dimensions={0} | all-to-all | bytes 786432 | tf_op jit(solution)/shard_map/all_to_all | solution.py:101
  320.8 0.8 copy.261
  (53 shorter events, 2.5 us)
Async XLA Ops:
  20.3 43.3 %all-to-all-start.1 = ((bf16[8,3,1,2,128,128]{5,4,3,1,2,0:T(8,128)(2,1)}), bf16[8,3,1,2,128,128]{5,4,3,1,2,0:T(8,128)(2,1)S(1)}, u32[]{:S(2)}, u32[]{:S(2)}) async-start(bf16[8,3,1,2,128,128]{5,4,3,1,2,0:T(8,128)(2,1)} %bitcast_dynamic-update-slice_fusion), calls=%async_computation.1 | async-start | bytes 3145728 | tf_op jit(solution)/shard_map/all_to_all | solution.py:13
  30.2 120.3 %all-reduce.10.cloned.1.call-start = ((), (), s32[]{:S(2)}) async-start(), calls=%async_computation.10 | async-start | bytes 6291456 | tf_op jit(solution)/shard_map/psum | solution.py:34
  66.4 84.2 %reduce-scatter.5.cloned.1.call-start = ((), (), s32[]{:S(2)}) async-start(), calls=%async_computation.8 | async-start | bytes 1769472 | tf_op jit(solution)/shard_map/reduce_scatter | solution.py:27
  67.0 138.2 %reduce-scatter.3.cloned.1.call-start = ((), (), s32[]{:S(2)}) async-start(), calls=%async_computation.6 | async-start | bytes 1769472 | tf_op jit(solution)/shard_map/reduce_scatter | solution.py:27
  67.6 188.8 %all-reduce.12.cloned.1.call-start = ((), (), s32[]{:S(2)}) async-start(), calls=%async_computation.11 | async-start | bytes 6291456 | tf_op jit(solution)/shard_map/psum | solution.py:34
  150.5 0.7 copy-start
  150.5 9.2 %copy-start.1 = (u32[256]{0:T(256)S(1)}, u32[256]{0:T(256)}, u32[]{:S(2)}) copy-start(u32[256]{0:T(256)} %constant.100) | copy-start | bytes 3076
  150.5 113.3 %all-gather.7.cloned.1.call-start = ((), (), s32[]{:S(2)}) async-start(), calls=%async_computation.9 | async-start | bytes 1769472 | tf_op jit(solution)/shard_map/all_gather | solution.py:28
  151.9 14.9 %all-to-all-start = ((s32[3,8,2]{0,2,1:T(2,128)}), s32[3,8,2]{0,2,1:T(2,128)S(1)}, u32[]{:S(2)}, u32[]{:S(2)}) async-start(s32[3,8,2]{0,2,1:T(2,128)} %copy.218), calls=%async_computation | async-start | bytes 16384 | tf_op jit(solution)/shard_map/all_to_all | solution.py:71
  159.7 114.4 %all-gather.5.cloned.1.call-start = ((), (), s32[]{:S(2)}) async-start(), calls=%async_computation.7 | async-start | bytes 1769472 | tf_op jit(solution)/shard_map/all_gather | solution.py:28
Sparse Core Ops, SparseCore 0:
  66.5 83.9 all-reduce.9
  153.1 103.1 all-reduce.11
Sparse Core Ops, SparseCore 1:
  69.4 43.9 reduce-scatter.4
  115.9 40.1 reduce-scatter.2
  157.7 63.6 all-gather.6
  223.3 50.8 all-gather.4
